TPU v7x, 32 devices: a whole 2x2x4 slice. The times are simulated.
32 devices in a mesh: dp: 4 (over y, x), space: 8 (over z, core).
Axes of the slice: x: 2, y: 2, z: 4, core: 2. Of those that a mesh axis runs over, the one named last changes fastest.
Arguments:
- fields: bfloat16 [4, 100, 32768], P('dp', None, 'space'), may hold values from -6 to 6
- cell_index: int32 [256, 128], P('space'), may hold values from 0 to 6143
- interp_weight: bfloat16 [256, 16, 128], P('space'), may hold values from 0 to 2, as said below
- w_in: bfloat16 [100, 1024], replicated, may hold values from -0.625 to 0.625
- ln_gain: float32 [1024], replicated, may hold values from 0.5 to 1.5
- w_qkv: bfloat16 [1024, 3072], P('dp'), may hold values from -0.1875 to 0.1875
- w_out: bfloat16 [1024, 1024], P('dp'), may hold values from -3 to 3
Outputs:
- latent: bfloat16 [4, 4096, 1024], P('dp', 'space')
- update: bfloat16 [4, 4096, 1024], P('dp', 'space')
Inputs may be any that keep to these rules, and one draw needn't show every extreme that they name: `interp_weight`: in each block the slots from some count on carry zero weight for all its 16 nodes; that count lies between 48 and 128. `cell_index`: indexes a shard's 4096 cells extended by 1024 cells of each neighbouring shard, lower neighbour first.
All inputs are finite; a program needn't handle non-finite values.
Results may differ from a plain program's by a relative error of at most 0.0068.
Values may be sent and summed in bfloat16 or wider, within the bound.
A program may use at most 128 MiB of HBM per device.

v0:
```python
import functools

import jax
import jax.numpy as jnp
from jax import lax
from jax.experimental import pallas as pl
from jax.experimental.pallas import tpu as pltpu
from jax.sharding import PartitionSpec as P

HEADS = 16
GROUP_HEADS = 4
F32, BF16 = jnp.float32, jnp.bfloat16
MESH = pl.DeviceIdType.MESH


def kernel(
    n, space, index_ref, field_ref, weight_ref, w_in_ref, gain_ref, w_qkv_ref, w_out_ref,
    att_out, w_out_full, enc_out,
    low_ref, high_ref, cells_ref, picked_ref, enc_ref, w_in_full, normed_ref, qkv_ref, out_ref,
    q_ref, k_ref, v_ref, att_ref,
    local_sem, leave_sem, field_send, field_recv, enc_send, enc_recv,
    a_send, a_recv, f_send, f_recv, p_send, p_recv,
):
    d, s = lax.axis_index("dp"), lax.axis_index("space")
    up, down = lax.rem(s + 1, space), lax.rem(s + space - 1, space)
    core = lax.rem(s, 2)
    partner = s + 1 - 2 * core
    channels, cell_count = field_ref.shape
    reach = low_ref.shape[1]
    rows = w_qkv_ref.shape[0]
    half = rows // 2
    quarter = half // 2
    width = w_out_ref.shape[1]
    groups, _, gw3 = qkv_ref.shape
    gw = gw3 // 3
    head_size = gw // GROUP_HEADS
    nodes = att_out.shape[0]
    margin = nodes // 2
    window = nodes + 2 * margin
    blocks, per_block, slots = weight_ref.shape
    if n == 4:
        peers = [d + 1 - 2 * lax.rem(d, 2), lax.rem(d + 2, 4), 3 - d]
    else:
        peers = [lax.rem(d + i, n) for i in range(1, n)]

    local = []
    for g in range(groups):
        for t in range(3):
            local.append(pltpu.make_async_copy(
                w_qkv_ref.at[:, pl.ds(t * width + g * gw, gw)],
                qkv_ref.at[g, pl.ds(pl.multiple_of(d * rows, rows), rows), pl.ds(t * gw, gw)],
                local_sem.at[len(local)]))
    local.append(pltpu.make_async_copy(
        w_out_ref, out_ref.at[pl.ds(pl.multiple_of(d * rows, rows), rows), :],
        local_sem.at[len(local)]))
    for copy in local:
        copy.start()

    barrier = pltpu.get_barrier_semaphore()
    for peer in peers:
        pl.semaphore_signal(barrier, inc=1, device_id=(peer, s), device_id_type=MESH)
    for peer in (up, down):
        pl.semaphore_signal(barrier, inc=1, device_id=(d, peer), device_id_type=MESH)
    pl.semaphore_wait(barrier, len(peers) + 2)

    def remote(src, dst, send, recv, device):
        return pltpu.make_async_remote_copy(
            src_ref=src, dst_ref=dst, send_sem=send, recv_sem=recv,
            device_id=device, device_id_type=MESH)

    field_up = remote(field_ref.at[:, pl.ds(cell_count - reach, reach)], low_ref,
                      field_send.at[0], field_recv.at[0], (d, up))
    field_down = remote(field_ref.at[:, pl.ds(0, reach)], high_ref,
                        field_send.at[1], field_recv.at[1], (d, down))
    field_up.start()
    field_down.start()

    def piece(c, slot, lo, size):
        span = pl.ds(pl.multiple_of(slot * rows + lo, size), size)
        return out_ref.at[span, :] if c == groups else qkv_ref.at[c, span, :]

    def own_copy(c, i):
        ref = piece(c, d, core * half, half)
        return remote(ref, ref, a_send.at[c, i], a_recv.at[c, i], (peers[i], s))

    def own_recv(c, i):
        source = peers[i] if n == 4 else peers[n - 2 - i]
        ref = piece(c, source, core * half, half)
        return remote(ref, ref, a_send.at[c, i], a_recv.at[c, i], (peers[i], s)), source

    def swap(c, i, slot, side):
        ref = piece(c, slot, side * half, half)
        return remote(ref, ref, p_send.at[c, i], p_recv.at[c, i], (d, partner))

    direct = 2 if n == 4 else n - 1

    def begin(c):
        mine = local[3 * c:3 * c + 3] if c < groups else local[-1:]
        for copy in mine:
            copy.wait()
        for i in range(direct):
            own_copy(c, i).start()

    def onward(c, i, slot):
        ref = piece(c, slot, core * half + i * quarter, quarter)
        return remote(ref, ref, f_send.at[c, i], f_recv.at[c, i], (peers[1 - i], s))

    def forward(c):
        for i in range(direct):
            copy, source = own_recv(c, i)
            copy.wait_recv()
            if n == 4:
                onward(c, i, source).start()
            swap(c, i, source, core).start()

    def finish(c):
        if n == 4:
            for i in range(2):
                onward(c, i, peers[2]).wait_recv()
            swap(c, 2, peers[2], core).start()
        for i in range(n - 1):
            source = peers[i] if n == 4 else peers[n - 2 - i]
            swap(c, i, source, 1 - core).wait_recv()

    def drain(c):
        for i in range(direct):
            own_copy(c, i).wait_send()
        if n == 4:
            for i in range(2):
                onward(c, i, peers[i]).wait_send()
        for i in range(n - 1):
            source = peers[i] if n == 4 else peers[n - 2 - i]
            swap(c, i, source, core).wait_send()

    begin(0)
    begin(1)
    begin(2)

    unit = (lax.broadcasted_iota(jnp.int32, (channels, 128), 0)
            == lax.broadcasted_iota(jnp.int32, (channels, 128), 1)).astype(BF16)

    def turn(source, start, target):
        cells_ref[pl.ds(target, 512), :] = lax.dot_general(
            source[:, pl.ds(start, 512)], unit, (((0,), (0,)), ((), ())),
            preferred_element_type=F32)

    @pl.loop(0, cell_count // 512, unroll=2)
    def _(i):
        turn(field_ref, pl.multiple_of(i * 512, 512), pl.multiple_of(reach + i * 512, 512))

    pad = w_in_full.shape[0]
    w_in_full[pl.ds(pad - 32, 32), :] = jnp.zeros((32, width), BF16)
    w_in_full[pl.ds(0, channels), :] = w_in_ref[...]

    field_up.wait_recv()
    field_down.wait_recv()

    @pl.loop(0, reach // 512)
    def _(i):
        turn(low_ref, pl.multiple_of(i * 512, 512), pl.multiple_of(i * 512, 512))
        turn(high_ref, pl.multiple_of(i * 512, 512),
             pl.multiple_of(reach + cell_count + i * 512, 512))

    def gather(first, last):
        @pl.loop(first, last)
        def _(b):
            base = pl.multiple_of(b * slots, slots)
            for j in range(slots):
                picked_ref[pl.ds(base + j, 1), :] = cells_ref[pl.ds(index_ref[b, j], 1), :]

    gather(0, blocks // 2)
    forward(0)
    begin(3)
    gather(blocks // 2, blocks)

    per_step = 8

    @pl.loop(0, blocks // per_step)
    def _(i):
        for j in range(per_step):
            b = i * per_step + j
            rows_b = picked_ref[pl.ds(pl.multiple_of(b * slots, slots), slots), :].astype(BF16)
            enc_ref[pl.ds(pl.multiple_of(margin + b * per_block, per_block), per_block), :] = jnp.dot(
                weight_ref[b], rows_b, preferred_element_type=F32).astype(BF16)

    enc_up = remote(enc_ref.at[pl.ds(nodes, margin), :], enc_ref.at[pl.ds(0, margin), :],
                    enc_send.at[0], enc_recv.at[0], (d, up))
    enc_down = remote(enc_ref.at[pl.ds(margin, margin), :],
                      enc_ref.at[pl.ds(margin + nodes, margin), :],
                      enc_send.at[1], enc_recv.at[1], (d, down))
    enc_up.start()
    enc_down.start()
    enc_leave = pltpu.make_async_copy(enc_ref.at[pl.ds(margin, nodes), :], enc_out, leave_sem.at[0])
    enc_leave.start()
    forward(1)

    def embed(start):
        embedded = jnp.dot(enc_ref[pl.ds(start, 128), :], w_in_full[...], preferred_element_type=F32)
        average = jnp.mean(embedded, axis=1, keepdims=True)
        centered = embedded - average
        spread = jnp.mean(centered * centered, axis=1, keepdims=True)
        normed_ref[pl.ds(start, 128), :] = (
            centered * lax.rsqrt(spread + 1e-05) * gain_ref[...]).astype(BF16)

    @pl.loop(0, nodes // 128, unroll=2)
    def _(i):
        embed(pl.multiple_of(margin + i * 128, 128))

    enc_up.wait_recv()
    enc_down.wait_recv()

    @pl.loop(0, margin // 128)
    def _(i):
        embed(pl.multiple_of(i * 128, 128))
        embed(pl.multiple_of(margin + nodes + i * 128, 128))

    forward(2)
    begin(groups)

    same_head = (lax.broadcasted_iota(jnp.int32, (gw, gw), 0) // head_size
                 == lax.broadcasted_iota(jnp.int32, (gw, gw), 1) // head_size).astype(BF16)
    contract_last = (((1,), (1,)), ((), ()))

    def unit_heads(block, scale):
        squares = block * block
        high = squares.astype(BF16)
        rest = (squares - high.astype(F32)).astype(BF16)
        total = (jnp.dot(high, same_head, preferred_element_type=F32)
                 + jnp.dot(rest, same_head, preferred_element_type=F32))
        return (block * lax.rsqrt(total * (1.0 / head_size) + 1e-06)).astype(BF16) * scale

    scale = jnp.asarray(head_size ** -0.5, BF16)
    one = jnp.asarray(1.0, BF16)

    def compute(g):
        for i in range(window // 512):
            span = pl.ds(i * 512, 512)
            part = jnp.dot(normed_ref[span, :], qkv_ref[g, :, pl.ds(gw, 2 * gw)],
                           preferred_element_type=F32)
            k_ref[span, :] = unit_heads(part[:, :gw], one)
            v_ref[span, :] = part[:, gw:].astype(BF16)
        part = jnp.dot(normed_ref[pl.ds(margin, nodes), :], qkv_ref[g, :, pl.ds(0, gw)],
                       preferred_element_type=F32)
        q_ref[...] = unit_heads(part, scale)

        @pl.loop(0, nodes // 128, unroll=2)
        def _(i):
            span = pl.ds(pl.multiple_of(i * 128, 128), 128)
            queries = q_ref[span, :]
            head_of = lax.broadcasted_iota(jnp.int32, (128, gw), 1) // head_size
            stacked = jnp.concatenate(
                [jnp.where(head_of == h, queries, jnp.zeros_like(queries))
                 for h in range(GROUP_HEADS)], axis=0)
            scores = lax.dot_general(stacked, k_ref[...], contract_last,
                                     preferred_element_type=F32)
            weights = jnp.exp(scores)
            total = jnp.sum(weights, axis=1, keepdims=True)
            out = jnp.dot(weights.astype(BF16), v_ref[...], preferred_element_type=F32)
            out = out * (1.0 / total)
            mixed = out[:128]
            for h in range(1, GROUP_HEADS):
                mixed = jnp.where(head_of == h, out[h * 128:(h + 1) * 128], mixed)
            att_ref[g, span, :] = mixed.astype(BF16)

    def leave(g):
        return pltpu.make_async_copy(
            att_ref.at[g], att_out.at[:, pl.ds(g * gw, gw)], leave_sem.at[2 + g])

    w_out_leave = pltpu.make_async_copy(out_ref, w_out_full, leave_sem.at[1])

    @pl.loop(0, groups)
    def _(g):
        for c in range(groups):
            @pl.when(g == c)
            def _():
                finish(c)
                if c == 0:
                    forward(groups - 1)
                if c == groups - 2:
                    forward(groups)
                if c:
                    leave(c - 1).start()
        compute(g)

    leave(groups - 1).start()
    finish(groups)
    w_out_leave.start()
    for g in range(groups):
        leave(g).wait()
    w_out_leave.wait()
    enc_leave.wait()
    for copy in (field_up, field_down, enc_up, enc_down):
        copy.wait_send()
    for c in range(groups + 1):
        drain(c)


def project(enc_ref, w_in_ref, att_ref, w_out_ref, latent_ref, update_ref):
    channels = w_in_ref.shape[0]
    latent_ref[...] = jnp.dot(enc_ref[:, :channels], w_in_ref[...],
                              preferred_element_type=F32).astype(BF16)
    update_ref[...] = jnp.dot(att_ref[...], w_out_ref[...],
                              preferred_element_type=F32).astype(BF16)


def shards(n, space, fields, cell_index, interp_weight, w_in, ln_gain, w_qkv, w_out):
    width = w_out.shape[1]
    blocks, per_block, _ = interp_weight.shape
    nodes = blocks * per_block
    channels, cells = fields.shape[1:]
    reach = cells // 4
    gw = width // HEADS * GROUP_HEADS
    groups = width // gw
    vmem = pl.BlockSpec(memory_space=pltpu.VMEM)
    hbm = pl.BlockSpec(memory_space=pl.ANY)
    dma = pltpu.SemaphoreType.DMA
    attended, w_out_full, encoded = pl.pallas_call(
        functools.partial(kernel, n, space),
        out_shape=[jax.ShapeDtypeStruct(shape, BF16)
                   for shape in ((nodes, width), (width, width), (nodes, 128))],
        in_specs=[pl.BlockSpec(memory_space=pltpu.SMEM), vmem, vmem, vmem, vmem, hbm, hbm],
        out_specs=[hbm, hbm, hbm],
        scratch_shapes=[
            pltpu.VMEM((channels, reach), BF16),
            pltpu.VMEM((channels, reach), BF16),
            pltpu.VMEM((cells + 2 * reach, 128), F32),
            pltpu.VMEM((blocks * 128, 128), F32),
            pltpu.VMEM((2 * nodes, 128), BF16),
            pltpu.VMEM((128, width), BF16),
            pltpu.VMEM((2 * nodes, width), BF16),
            pltpu.VMEM((groups, width, 3 * gw), BF16),
            pltpu.VMEM((width, width), BF16),
            pltpu.VMEM((nodes, gw), BF16),
            pltpu.VMEM((2 * nodes, gw), BF16),
            pltpu.VMEM((2 * nodes, gw), BF16),
            pltpu.VMEM((groups, nodes, gw), BF16),
            dma((3 * groups + 1,)), dma((groups + 2,)),
            dma((2,)), dma((2,)), dma((2,)), dma((2,)),
            dma((groups + 1, n - 1)), dma((groups + 1, n - 1)),
            dma((groups + 1, 2)), dma((groups + 1, 2)),
            dma((groups + 1, n - 1)), dma((groups + 1, n - 1)),
        ],
        compiler_params=pltpu.CompilerParams(
            collective_id=0, has_side_effects=True, vmem_limit_bytes=60 * 2**20),
    )(cell_index, fields[0], interp_weight, w_in, ln_gain[None], w_qkv, w_out)
    step = nodes // 2

    def by_row(size):
        return pl.BlockSpec((step, size), lambda i: (i, 0))

    def whole(array):
        return pl.BlockSpec(array.shape, lambda i: (0, 0))

    latent, update = pl.pallas_call(
        project,
        grid=(nodes // step,),
        out_shape=[jax.ShapeDtypeStruct((nodes, width), BF16)] * 2,
        in_specs=[by_row(128), whole(w_in), by_row(width), whole(w_out_full)],
        out_specs=[by_row(width), by_row(width)],
    )(encoded, w_in, attended, w_out_full)
    return latent[None], update[None]


def solution(mesh):
    placed = (
        P("dp", None, "space"),
        P("space", None),
        P("space", None, None),
        P(),
        P(),
        P("dp", None),
        P("dp", None),
    )
    return jax.shard_map(
        functools.partial(shards, mesh.shape["dp"], mesh.shape["space"]),
        mesh=mesh,
        in_specs=placed,
        out_specs=(P("dp", "space", None), P("dp", "space", None)),
        check_vma=False,
    )
```

profile of v0, /device:TPU:0, one launch (start us, length us, event | category | flops | bytes accessed | tf_op | source)
XLA Modules:
  0.0 60.4 jit_solution(13374163640674630027)
XLA Ops:
  0.6 55.4 %shard_map.86 = (bf16[512,1024]{1,0:T(8,128)(2,1)}, bf16[1024,1024]{1,0:T(8,128)(2,1)}, bf16[512,128]{1,0:T(8,128)(2,1)}) custom-call(s32[32,128]{1,0:T(8,128)} %index_ref.1, bf16[100,4096]{1,0:T(8,128)(2,1)} %bitcast.4, bf16[32,16,128]{2,1,0:T(8,128)(2,1)} %weight_ref.1, bf16[100,1024]{1,0:T(8,128)(2,1)} %w_in_ref.3, f32[1,1024]{1,0:T(1,128)} %bitcast.5, ...), custom_call_target="tpu_custom_call" | custom-call | tf_op jit(solution)/shard_map/pallas_call | solution.py:317
  56.1 4.4 %shard_map.87 = (bf16[512,1024]{1,0:T(8,128)(2,1)}, bf16[512,1024]{1,0:T(8,128)(2,1)}) custom-call(bf16[512,128]{1,0:T(8,128)(2,1)} %get-tuple-element.7.enc_ref, bf16[100,1024]{1,0:T(8,128)(2,1)} %w_in_ref.3, bf16[512,1024]{1,0:T(8,128)(2,1)} %get-tuple-element.8.att_ref, bf16[1024,1024]{1,0:T(8,128)(2,1)} %get-tuple-element.9.w_out_ref), custom_call_target="tpu_custom_call" | custom-call | tf_op jit(solution)/shard_map/pallas_call | solution.py:354
where the time goes:
time: 60.6 us; the launch traced here: 60.4 us
  Pallas kernels  59.8 us (99%)
  between operations  0.64 us (1%)
    pallas_call x1, Pallas kernels, shards(): pl.pallas_call(functools.partial(kernel, n, space), out_shape=[jax.ShapeD...  55.4 us
    pallas_call x1, Pallas kernels, shards(): pl.pallas_call(project, grid=(nodes // step,), out_shape=[jax.ShapeDtypeS...  4.36 us

commit v1 on v0

v1 whole, which is shorter than its diff:
```python
import functools

import jax
import jax.numpy as jnp
from jax import lax
from jax.experimental import pallas as pl
from jax.experimental.pallas import tpu as pltpu
from jax.sharding import PartitionSpec as P

HEADS = 16
GROUP_HEADS = 4
F32, BF16 = jnp.float32, jnp.bfloat16
MESH = pl.DeviceIdType.MESH
CONTRACT_LAST = (((1,), (1,)), ((), ()))


def kernel(
    n, space, index_hbm, field_hbm, weight_hbm, w_in_hbm, gain_hbm, w_qkv_hbm, w_out_hbm,
    att_ref, wo_ref, enc_out, w_in_full,
    index_ref, field_ref, weight_ref, w_in_ref, gain_ref,
    low_ref, high_ref, cells_ref, picked_ref, enc_ref, normed_ref, wq_ref,
    q_ref, k_ref, vt_ref,
    in_sem, local_sem, field_send, field_recv, enc_send, enc_recv, norm_send, norm_recv,
    a_send, a_recv, z_send, z_recv, swap_send, swap_recv, give_send, give_recv,
):
    d, s = lax.axis_index("dp"), lax.axis_index("space")
    up, down = lax.rem(s + 1, space), lax.rem(s + space - 1, space)
    core = lax.rem(s, 2)
    partner = s + 1 - 2 * core
    outer = lax.rem(s + space - 1 + 2 * core, space)
    layer = lax.rem(s // 2, 2)
    beside = s + 2 - 4 * layer
    share = n == 4 and space % 4 == 0
    channels, cell_count = field_ref.shape
    reach = low_ref.shape[1]
    rows, width = w_out_hbm.shape
    gw = q_ref.shape[1]
    parts = width // gw
    groups = parts // 2
    chunks = 3 * groups + parts // 2
    head_size = gw // GROUP_HEADS
    nodes = enc_out.shape[0]
    margin = nodes // 2
    side = nodes + margin
    window = nodes + 2 * margin
    blocks, per_block, slots = weight_ref.shape
    if n == 4:
        peers = [d + 1 - 2 * lax.rem(d, 2), lax.rem(d + 2, 4), 3 - d]
    else:
        peers = [lax.rem(d + i, n) for i in range(1, n)]

    def source_of(i):
        return peers[i] if n == 4 else peers[n - 2 - i]

    barrier = pltpu.get_barrier_semaphore()
    for peer in peers:
        pl.semaphore_signal(barrier, inc=1, device_id=(peer, s), device_id_type=MESH)
    near = (up, down, beside) if share else (up, down)
    for peer in near:
        pl.semaphore_signal(barrier, inc=1, device_id=(d, peer), device_id_type=MESH)

    inputs = [
        pltpu.make_async_copy(source, target, in_sem.at[i])
        for i, (source, target) in enumerate((
            (field_hbm, field_ref), (index_hbm, index_ref), (weight_hbm, weight_ref),
            (w_in_hbm, w_in_ref), (gain_hbm, gain_ref)))
    ]
    for copy in inputs:
        copy.start()

    def chunk(c):
        return wq_ref.at[c] if c < 3 * groups else wo_ref.at[groups * core + c - 3 * groups]

    own = pl.ds(pl.multiple_of(d * rows, rows), rows)
    order = [3 * g + t for g in range(groups) for t in (1, 0, 2)]
    order += range(3 * groups, chunks)
    local = {}
    for c in order:
        if c < 3 * groups:
            column = c % 3 * width + (core * groups + c // 3) * gw
            source = w_qkv_hbm.at[:, pl.ds(pl.multiple_of(column, gw), gw)]
        else:
            column = (core * groups + c - 3 * groups) * gw
            source = w_out_hbm.at[:, pl.ds(pl.multiple_of(column, gw), gw)]
        local[c] = pltpu.make_async_copy(source, chunk(c).at[own, :], local_sem.at[c])
        local[c].start()

    def remote(src, dst, send, recv, device):
        return pltpu.make_async_remote_copy(
            src_ref=src, dst_ref=dst, send_sem=send, recv_sem=recv,
            device_id=device, device_id_type=MESH)

    field_up = remote(field_ref.at[:, pl.ds(cell_count - reach, reach)], low_ref,
                      field_send.at[0], field_recv.at[0], (d, up))
    field_down = remote(field_ref.at[:, pl.ds(0, reach)], high_ref,
                        field_send.at[1], field_recv.at[1], (d, down))

    whole = rows * 11 // 256 * 16
    half = rows // 2

    def span(c, i, mine):
        if not share:
            return 0, rows
        at = layer if mine else 1 - layer
        if i == 2:
            return at * half, half
        return at * (rows - whole), whole

    def passed(c, i, mine):
        at = layer if mine else 1 - layer
        if i == 2:
            return at * half, half
        return at * whole, rows - whole

    def block(c, owner, lo, size):
        return chunk(c).at[pl.ds(pl.multiple_of(owner * rows + lo, 16), size), :]

    def direct(c, i, owner):
        ref = block(c, owner, *span(c, i, True))
        return remote(ref, ref, a_send.at[c, i], a_recv.at[c, i], (peers[i], s))

    def onward(c, i, mine):
        ref = block(c, source_of(i), *passed(c, i, mine))
        return remote(ref, ref, z_send.at[c, i], z_recv.at[c, i], (d, beside))

    def begin(c):
        local[c].wait()
        for i in range(n - 1):
            direct(c, i, d).start()

    def relay(c):
        if share:
            for i in range(n - 1):
                direct(c, i, source_of(i)).wait_recv()
                onward(c, i, True).start()

    def finish(c):
        for i in range(n - 1):
            if share:
                onward(c, i, False).wait_recv()
            else:
                direct(c, i, source_of(i)).wait_recv()

    def swap(j):
        ref = wo_ref.at[j]
        at = lax.rem(j, groups)
        return remote(ref, ref, swap_send.at[at], swap_recv.at[at], (d, partner))

    pl.semaphore_wait(barrier, len(peers) + len(near))
    inputs[0].wait()
    field_up.start()
    field_down.start()
    for c in order:
        begin(c)

    unit = (lax.broadcasted_iota(jnp.int32, (channels, 128), 0)
            == lax.broadcasted_iota(jnp.int32, (channels, 128), 1)).astype(BF16)

    def turn(source, start, target):
        cells_ref[pl.ds(target, 512), :] = lax.dot_general(
            source[:, pl.ds(start, 512)], unit, (((0,), (0,)), ((), ())),
            preferred_element_type=F32)

    @pl.loop(0, cell_count // 512, unroll=2)
    def _(i):
        turn(field_ref, pl.multiple_of(i * 512, 512), pl.multiple_of(reach + i * 512, 512))

    for copy in inputs[1:]:
        copy.wait()
    pad = w_in_full.shape[0]
    w_in_full[pl.ds(pad - 32, 32), :] = jnp.zeros((32, width), BF16)
    w_in_full[pl.ds(0, channels), :] = w_in_ref[...]

    field_up.wait_recv()
    field_down.wait_recv()

    @pl.loop(0, reach // 512)
    def _(i):
        turn(low_ref, pl.multiple_of(i * 512, 512), pl.multiple_of(i * 512, 512))
        turn(high_ref, pl.multiple_of(i * 512, 512),
             pl.multiple_of(reach + cell_count + i * 512, 512))

    def gather(first, last):
        @pl.loop(first, last)
        def _(b):
            base = pl.multiple_of(b * slots, slots)
            for j in range(slots):
                picked_ref[pl.ds(base + j, 1), :] = cells_ref[pl.ds(index_ref[b, j], 1), :]

    gather(0, blocks // 2)
    relay(order[0])
    gather(blocks // 2, blocks)
    relay(order[1])

    own_base = margin + core * nodes
    own_edge = core * (nodes + margin)
    far_edge = (1 - core) * (nodes + margin)
    own_halo = core * (margin + 2 * nodes)
    far_halo = (1 - core) * (margin + 2 * nodes)
    far_base = margin + (1 - core) * nodes
    per_step = 8

    @pl.loop(0, blocks // per_step)
    def _(i):
        for j in range(per_step):
            b = i * per_step + j
            rows_b = picked_ref[pl.ds(pl.multiple_of(b * slots, slots), slots), :].astype(BF16)
            encoded = jnp.dot(weight_ref[b], rows_b, preferred_element_type=F32).astype(BF16)
            start = pl.multiple_of(b * per_block, per_block)
            enc_out[pl.ds(start, per_block), :] = encoded
            enc_ref[pl.ds(pl.multiple_of(own_base + start, per_block), per_block), :] = encoded

    def enc_copy(target):
        edge = pl.multiple_of(margin + own_edge, margin)
        return remote(enc_ref.at[pl.ds(edge, margin), :],
                      enc_ref.at[pl.ds(pl.multiple_of(target, margin), margin), :],
                      enc_send.at[0], enc_recv.at[0], (d, outer))

    enc_copy(far_halo).start()

    def embed(start):
        embedded = jnp.dot(enc_ref[pl.ds(start, 128), :], w_in_full[...], preferred_element_type=F32)
        average = jnp.mean(embedded, axis=1, keepdims=True)
        centered = embedded - average
        spread = jnp.mean(centered * centered, axis=1, keepdims=True)
        normed_ref[pl.ds(start, 128), :] = (
            centered * lax.rsqrt(spread + 1e-05) * gain_ref[...]).astype(BF16)

    def norm_copy(i, start, size):
        ref = normed_ref.at[pl.ds(pl.multiple_of(start, margin), size), :]
        return remote(ref, ref, norm_send.at[i], norm_recv.at[i], (d, partner))

    @pl.loop(0, nodes // 128, unroll=2)
    def _(i):
        embed(pl.multiple_of(own_base + i * 128, 128))

    norm_copy(0, own_base, nodes).start()
    relay(order[2])
    enc_copy(own_halo).wait_recv()

    @pl.loop(0, margin // 128, unroll=2)
    def _(i):
        embed(pl.multiple_of(own_halo + i * 128, 128))

    norm_copy(1, own_halo, margin).start()

    same_head = (lax.broadcasted_iota(jnp.int32, (gw, gw), 0) // head_size
                 == lax.broadcasted_iota(jnp.int32, (gw, gw), 1) // head_size).astype(BF16)

    def unit_heads(values):
        total = jnp.dot((values * values).astype(BF16), same_head, preferred_element_type=F32)
        return (values * lax.rsqrt(total * (1.0 / head_size) + 1e-06)).astype(BF16)

    scale = jnp.asarray(head_size ** -0.5, BF16)

    def project_part(start, size, c):
        return jnp.dot(normed_ref[pl.ds(start, size), :], wq_ref[c], preferred_element_type=F32)

    def keys(g, start):
        start = pl.multiple_of(start, margin)
        k_ref[pl.ds(start, side), :] = unit_heads(project_part(start, side, 3 * g + 1))

    def queries(g, i):
        q_ref[pl.ds(i * nodes, nodes), :] = unit_heads(
            project_part(margin + i * nodes, nodes, 3 * g)) * scale

    def values(g, start):
        start = pl.multiple_of(start, margin)
        vt_ref[:, pl.ds(start, side)] = project_part(start, side, 3 * g + 2).astype(BF16).T

    head_of = lax.broadcasted_iota(jnp.int32, (nodes, gw), 1) // head_size

    def attend(t, slot):
        start = pl.multiple_of(t * nodes, nodes)
        asked = q_ref[pl.ds(start, nodes), :]
        seen = pl.ds(start, window)

        def score(h):
            picked = jnp.where(head_of == h, asked, jnp.zeros_like(asked))
            return lax.dot_general(k_ref[seen, :], picked, CONTRACT_LAST, preferred_element_type=F32)

        outs = []
        scores = score(0)
        for h in range(GROUP_HEADS):
            weights = jnp.exp(scores)
            if h + 1 < GROUP_HEADS:
                scores = score(h + 1)
            total = jnp.sum(weights, axis=0, keepdims=True)
            out = jnp.dot(vt_ref[pl.ds(h * head_size, head_size), seen], weights.astype(BF16),
                          preferred_element_type=F32)
            outs.append(out * (1.0 / total))
        att_ref[slot] = jnp.concatenate(outs, axis=0).astype(BF16).T

    def give(g, mine):
        at = core * groups + g if mine else (1 - core) * groups + g
        return remote(att_ref.at[parts + g], att_ref.at[at], give_send.at[g], give_recv.at[g],
                      (d, partner))

    def at_group(g, value, action):
        @pl.when(g == value)
        def _():
            action()

    @pl.loop(0, groups)
    def _(g):
        for value in range(groups):
            at_group(g, value, lambda: finish(3 * value + 1))
        keys(g, own_edge)

        @pl.when(g == 0)
        def _():
            norm_copy(0, far_base, nodes).wait_recv()
            norm_copy(1, far_halo, margin).wait_recv()

        keys(g, far_edge)
        for value in range(groups):
            at_group(g, value, lambda: finish(3 * value))
        for i in range(2):
            queries(g, i)
        at_group(g, 0, lambda: relay(order[3]))
        for value in range(groups):
            at_group(g, value, lambda: finish(3 * value + 2))
        values(g, own_edge)
        values(g, far_edge)
        at_group(g, 1, lambda: relay(order[6]))

        @pl.loop(0, 2)
        def _(i):
            t = jnp.where(i == 0, 1 - core, core)
            attend(t, jnp.where(i == 0, parts + g, core * groups + g))

            @pl.when(i == 0)
            def _():
                for value in range(groups):
                    at_group(g, value, lambda: give(value, True).start())

                at_group(g, 0, lambda: relay(order[4]))

                @pl.when(g == groups - 1)
                def _():
                    relay(order[7])
                    finish(order[6])
                    swap(groups * core).start()

            @pl.when((i == 1) & (g == 0))
            def _():
                relay(order[5])

    finish(order[7])
    swap(groups * core + 1).start()
    for g in range(groups):
        give(g, False).wait_recv()
        swap(groups * (1 - core) + g).wait_recv()
    for copy in (field_up, field_down, enc_copy(far_halo), norm_copy(0, own_base, nodes),
                 norm_copy(1, own_halo, margin)):
        copy.wait_send()
    for g in range(groups):
        give(g, True).wait_send()
        swap(groups * core + g).wait_send()
    for c in order:
        for i in range(n - 1):
            direct(c, i, d).wait_send()
            if share:
                onward(c, i, True).wait_send()


def project(enc_ref, w_in_ref, att_ref, w_out_ref, latent_hbm, update_hbm,
            latent_ref, update_ref, latent_sem, update_sem):
    parts, _, gw = w_out_ref.shape
    half = enc_ref.shape[0] // 2
    copies = []
    for i in range(2):
        span = pl.ds(i * half, half)
        latent_ref[span, :] = jnp.dot(
            enc_ref[span, :], w_in_ref[...], preferred_element_type=F32).astype(BF16)
        copies.append(pltpu.make_async_copy(
            latent_ref.at[span, :], latent_hbm.at[span, :], latent_sem.at[i]))
        copies[-1].start()
    for j in range(parts):
        update_ref[j] = sum(
            jnp.dot(att_ref[g], w_out_ref[j, pl.ds(g * gw, gw), :], preferred_element_type=F32)
            for g in range(parts)).astype(BF16)
        copies.append(pltpu.make_async_copy(
            update_ref.at[j], update_hbm.at[:, pl.ds(j * gw, gw)], update_sem.at[j]))
        copies[-1].start()
    for copy in copies:
        copy.wait()


def shards(n, space, fields, cell_index, interp_weight, w_in, ln_gain, w_qkv, w_out):
    width = w_out.shape[1]
    blocks, per_block, _ = interp_weight.shape
    nodes = blocks * per_block
    channels, cells = fields.shape[1:]
    reach = cells // 4
    gw = width // HEADS * GROUP_HEADS
    parts = width // gw
    groups = parts // 2
    chunks = 3 * groups + parts // 2
    vmem = pl.BlockSpec(memory_space=pltpu.VMEM)
    hbm = pl.BlockSpec(memory_space=pl.ANY)
    dma = pltpu.SemaphoreType.DMA
    attended, w_out_full, encoded, w_in_full = pl.pallas_call(
        functools.partial(kernel, n, space),
        out_shape=[pltpu.VMEM(shape, BF16)
                   for shape in ((parts + groups, nodes, gw), (parts, width, gw),
                                 (nodes, 128), (128, width))],
        in_specs=[hbm] * 7,
        out_specs=[vmem] * 4,
        scratch_shapes=[
            pltpu.SMEM(cell_index.shape, jnp.int32),
            pltpu.VMEM((channels, cells), BF16),
            pltpu.VMEM(interp_weight.shape, BF16),
            pltpu.VMEM(w_in.shape, BF16),
            pltpu.VMEM((1, width), F32),
            pltpu.VMEM((channels, reach), BF16),
            pltpu.VMEM((channels, reach), BF16),
            pltpu.VMEM((cells + 2 * reach, 128), F32),
            pltpu.VMEM((blocks * 128, 128), F32),
            pltpu.VMEM((3 * nodes, 128), BF16),
            pltpu.VMEM((3 * nodes, width), BF16),
            pltpu.VMEM((3 * groups, width, gw), BF16),
            pltpu.VMEM((2 * nodes, gw), BF16),
            pltpu.VMEM((3 * nodes, gw), BF16),
            pltpu.VMEM((gw, 3 * nodes), BF16),
            dma((5,)), dma((chunks,)),
            dma((2,)), dma((2,)), dma((1,)), dma((1,)), dma((2,)), dma((2,)),
            dma((chunks, n - 1)), dma((chunks, n - 1)),
            dma((chunks, 3)), dma((chunks, 3)),
            dma((groups,)), dma((groups,)), dma((groups,)), dma((groups,)),
        ],
        compiler_params=pltpu.CompilerParams(
            collective_id=0, has_side_effects=True, vmem_limit_bytes=40 * 2**20),
    )(*[pltpu.with_memory_space_constraint(array, pltpu.HBM) for array in (
        cell_index, fields[0], interp_weight, w_in, ln_gain[None], w_qkv, w_out)])

    operands = [pltpu.with_memory_space_constraint(array, pltpu.VMEM)
                for array in (encoded, w_in_full, attended, w_out_full)]
    latent, update = pl.pallas_call(
        project,
        out_shape=[jax.ShapeDtypeStruct((nodes, width), BF16)] * 2,
        in_specs=[vmem] * 4,
        out_specs=[hbm] * 2,
        scratch_shapes=[
            pltpu.VMEM((nodes, width), BF16), pltpu.VMEM((parts, nodes, gw), BF16),
            dma((2,)), dma((parts,)),
        ],
        compiler_params=pltpu.CompilerParams(vmem_limit_bytes=16 * 2**20),
    )(*operands)
    return latent[None], update[None]


def solution(mesh):
    placed = (
        P("dp", None, "space"),
        P("space", None),
        P("space", None, None),
        P(),
        P(),
        P("dp", None),
        P("dp", None),
    )
    return jax.shard_map(
        functools.partial(shards, mesh.shape["dp"], mesh.shape["space"]),
        mesh=mesh,
        in_specs=placed,
        out_specs=(P("dp", "space", None), P("dp", "space", None)),
        check_vma=False,
    )
```

time: 60.6 us -> 54.1 us (0.89)
  Pallas kernels: 59.8 us -> 53.4 us
    pallas_call x2, Pallas kernels: 59.8 us -> 53.4 us  [the longest x1 51 us: shards(): pl.pallas_call(functools.partial(kernel, n, space), out_shape=[pltpu.VMEM...]
where the time goes in v1:
time: 54.1 us; the launch traced here: 54 us
  Pallas kernels  53.4 us (99%)
  between operations  0.64 us (1%)
    pallas_call x1, Pallas kernels, shards(): pl.pallas_call(functools.partial(kernel, n, space), out_shape=[pltpu.VMEM...  51 us
    pallas_call x1, Pallas kernels, shards(): pl.pallas_call(project, out_shape=[jax.ShapeDtypeStruct((nodes, width), B...  2.37 us

profile of v1, /device:TPU:0, one launch (start us, length us, event | category | flops | bytes accessed | tf_op | source)
XLA Modules:
  0.0 54.0 jit_solution(16114924453610072113)
XLA Ops:
  0.6 51.0 %shard_map.86 = (bf16[6,512,256]{2,1,0:T(8,128)(2,1)S(1)}, bf16[4,1024,256]{2,1,0:T(8,128)(2,1)S(1)}, bf16[512,128]{1,0:T(8,128)(2,1)S(1)}, bf16[128,1024]{1,0:T(8,128)(2,1)S(1)}) custom-call(s32[32,128]{1,0:T(8,128)} %index_hbm.1, bf16[100,4096]{1,0:T(8,128)(2,1)} %bitcast.4, bf16[32,16,128]{2,1,0:T(8,128)(2,1)} %weight_hbm.1, bf16[100,1024]{1,0:T(8,128)(2,1)} %w_in_hbm.1, ...), custom_call_target="tpu_custom_call" | custom-call | tf_op jit(solution)/shard_map/pallas_call | solution.py:403
  51.6 2.4 %shard_map.87 = (bf16[512,1024]{1,0:T(8,128)(2,1)}, bf16[512,1024]{1,0:T(8,128)(2,1)}) custom-call(bf16[512,128]{1,0:T(8,128)(2,1)S(1)} %get-tuple-element.8.enc_ref, bf16[128,1024]{1,0:T(8,128)(2,1)S(1)} %get-tuple-element.9.w_in_ref, bf16[6,512,256]{2,1,0:T(8,128)(2,1)S(1)} %get-tuple-element.10.att_ref, bf16[4,1024,256]{2,1,0:T(8,128)(2,1)S(1)} %get-tuple-element.11.w_out_ref), custom_call_target="tpu_custom_call" | custom-call | tf_op jit(solution)/shard_map/pallas_call | solution.py:439

commit v2 on v1

--- a/solution.py
+++ b/solution.py
@@ -11,15 +11,16 @@
 GROUP_HEADS = 4
 F32, BF16 = jnp.float32, jnp.bfloat16
 MESH = pl.DeviceIdType.MESH
+SHARED = (2, 2, 2, 2, 2, 1, 2, 0)
 CONTRACT_LAST = (((1,), (1,)), ((), ()))
 
 
 def kernel(
     n, space, index_hbm, field_hbm, weight_hbm, w_in_hbm, gain_hbm, w_qkv_hbm, w_out_hbm,
-    att_ref, wo_ref, enc_out, w_in_full,
+    latent_ref, update_ref,
     index_ref, field_ref, weight_ref, w_in_ref, gain_ref,
-    low_ref, high_ref, cells_ref, picked_ref, enc_ref, normed_ref, wq_ref,
-    q_ref, k_ref, vt_ref,
+    low_ref, high_ref, cells_ref, picked_ref, enc_ref, w_in_full, normed_ref, wq_ref,
+    q_ref, k_ref, vt_ref, att_ref, wo_ref,
     in_sem, local_sem, field_send, field_recv, enc_send, enc_recv, norm_send, norm_recv,
     a_send, a_recv, z_send, z_recv, swap_send, swap_recv, give_send, give_recv,
 ):
@@ -39,9 +40,8 @@
     groups = parts // 2
     chunks = 3 * groups + parts // 2
     head_size = gw // GROUP_HEADS
-    nodes = enc_out.shape[0]
+    nodes = latent_ref.shape[0]
     margin = nodes // 2
-    side = nodes + margin
     window = nodes + 2 * margin
     blocks, per_block, slots = weight_ref.shape
     if n == 4:
@@ -98,48 +98,58 @@
     whole = rows * 11 // 256 * 16
     half = rows // 2
 
-    def span(c, i, mine):
-        if not share:
-            return 0, rows
-        at = layer if mine else 1 - layer
-        if i == 2:
-            return at * half, half
-        return at * (rows - whole), whole
-
-    def passed(c, i, mine):
-        at = layer if mine else 1 - layer
-        if i == 2:
-            return at * half, half
-        return at * whole, rows - whole
+    level = {c: SHARED[at] if share else 0 for at, c in enumerate(order)}
+
+    def span(c, i):
+        if i == 2 and level[c]:
+            return layer * half, half
+        if level[c] == 2:
+            return layer * (rows - whole), whole
+        return 0, rows
+
+    def passed(c, i):
+        if i == 2 and level[c]:
+            return layer * half, half
+        return layer * whole, rows - whole
+
+    def relayed(c):
+        return [(), (2,), (0, 1, 2)][level[c]]
 
     def block(c, owner, lo, size):
         return chunk(c).at[pl.ds(pl.multiple_of(owner * rows + lo, 16), size), :]
 
-    def direct(c, i, owner):
-        ref = block(c, owner, *span(c, i, True))
-        return remote(ref, ref, a_send.at[c, i], a_recv.at[c, i], (peers[i], s))
-
-    def onward(c, i, mine):
-        ref = block(c, source_of(i), *passed(c, i, mine))
-        return remote(ref, ref, z_send.at[c, i], z_recv.at[c, i], (d, beside))
+    def direct(c, i):
+        ref = block(c, d, *span(c, i))
+        return remote(ref, ref, a_send.at[c], a_recv.at[c], (peers[i], s))
+
+    def onward(c, i):
+        ref = block(c, source_of(i), *passed(c, i))
+        return remote(ref, ref, z_send.at[c], z_recv.at[c], (d, beside))
+
+    def all_direct(c):
+        ref = chunk(c).at[pl.ds(0, sum(span(c, i)[1] for i in range(n - 1))), :]
+        return remote(ref, ref, a_send.at[c], a_recv.at[c], (peers[0], s))
+
+    def all_onward(c):
+        ref = chunk(c).at[pl.ds(0, sum(passed(c, i)[1] for i in relayed(c))), :]
+        return remote(ref, ref, z_send.at[c], z_recv.at[c], (d, beside))
 
     def begin(c):
         local[c].wait()
         for i in range(n - 1):
-            direct(c, i, d).start()
+            direct(c, i).start()
 
     def relay(c):
-        if share:
-            for i in range(n - 1):
-                direct(c, i, source_of(i)).wait_recv()
-                onward(c, i, True).start()
+        if level[c]:
+            all_direct(c).wait_recv()
+            for i in relayed(c):
+                onward(c, i).start()
 
     def finish(c):
-        for i in range(n - 1):
-            if share:
-                onward(c, i, False).wait_recv()
-            else:
-                direct(c, i, source_of(i)).wait_recv()
+        if level[c]:
+            all_onward(c).wait_recv()
+        else:
+            all_direct(c).wait_recv()
 
     def swap(j):
         ref = wo_ref.at[j]
@@ -173,6 +183,7 @@
 
     field_up.wait_recv()
     field_down.wait_recv()
+    relay(order[0])
 
     @pl.loop(0, reach // 512)
     def _(i):
@@ -188,9 +199,8 @@
                 picked_ref[pl.ds(base + j, 1), :] = cells_ref[pl.ds(index_ref[b, j], 1), :]
 
     gather(0, blocks // 2)
-    relay(order[0])
+    relay(order[1])
     gather(blocks // 2, blocks)
-    relay(order[1])
 
     own_base = margin + core * nodes
     own_edge = core * (nodes + margin)
@@ -207,7 +217,6 @@
             rows_b = picked_ref[pl.ds(pl.multiple_of(b * slots, slots), slots), :].astype(BF16)
             encoded = jnp.dot(weight_ref[b], rows_b, preferred_element_type=F32).astype(BF16)
             start = pl.multiple_of(b * per_block, per_block)
-            enc_out[pl.ds(start, per_block), :] = encoded
             enc_ref[pl.ds(pl.multiple_of(own_base + start, per_block), per_block), :] = encoded
 
     def enc_copy(target):
@@ -230,19 +239,27 @@
         ref = normed_ref.at[pl.ds(pl.multiple_of(start, margin), size), :]
         return remote(ref, ref, norm_send.at[i], norm_recv.at[i], (d, partner))
 
-    @pl.loop(0, nodes // 128, unroll=2)
-    def _(i):
-        embed(pl.multiple_of(own_base + i * 128, 128))
-
-    norm_copy(0, own_base, nodes).start()
+    for half_at in range(2):
+        @pl.loop(0, margin // 128, unroll=2)
+        def _(i):
+            embed(pl.multiple_of(own_base + half_at * margin + i * 128, 128))
+
+        norm_copy(half_at, own_base + half_at * margin, margin).start()
+
     relay(order[2])
-    enc_copy(own_halo).wait_recv()
-
-    @pl.loop(0, margin // 128, unroll=2)
-    def _(i):
-        embed(pl.multiple_of(own_halo + i * 128, 128))
-
-    norm_copy(1, own_halo, margin).start()
+    for half_at in range(2):
+        latent_ref[pl.ds(half_at * margin, margin), :] = jnp.dot(
+            enc_ref[pl.ds(pl.multiple_of(own_base + half_at * margin, margin), margin), :],
+            w_in_full[...], preferred_element_type=F32).astype(BF16)
+
+    def embed_halo():
+        enc_copy(own_halo).wait_recv()
+
+        @pl.loop(0, margin // 128, unroll=2)
+        def _(i):
+            embed(pl.multiple_of(own_halo + i * 128, 128))
+
+        norm_copy(2, own_halo, margin).start()
 
     same_head = (lax.broadcasted_iota(jnp.int32, (gw, gw), 0) // head_size
                  == lax.broadcasted_iota(jnp.int32, (gw, gw), 1) // head_size).astype(BF16)
@@ -254,19 +271,30 @@
     scale = jnp.asarray(head_size ** -0.5, BF16)
 
     def project_part(start, size, c):
+        if not isinstance(start, int):
+            start = pl.multiple_of(start, margin)
         return jnp.dot(normed_ref[pl.ds(start, size), :], wq_ref[c], preferred_element_type=F32)
 
-    def keys(g, start):
-        start = pl.multiple_of(start, margin)
-        k_ref[pl.ds(start, side), :] = unit_heads(project_part(start, side, 3 * g + 1))
-
-    def queries(g, i):
-        q_ref[pl.ds(i * nodes, nodes), :] = unit_heads(
-            project_part(margin + i * nodes, nodes, 3 * g)) * scale
-
-    def values(g, start):
-        start = pl.multiple_of(start, margin)
-        vt_ref[:, pl.ds(start, side)] = project_part(start, side, 3 * g + 2).astype(BF16).T
+    def run(g, steps):
+        def product(kind, start, size):
+            return project_part(start, size, 3 * g + kind)
+
+        later = product(*steps[0])
+        for i, (kind, start, size) in enumerate(steps):
+            part = later
+            if i + 1 < len(steps):
+                later = product(*steps[i + 1])
+            if not isinstance(start, int):
+                start = pl.multiple_of(start, margin)
+            if kind == 0:
+                q_ref[pl.ds(start - margin, size), :] = unit_heads(part) * scale
+            elif kind == 1:
+                k_ref[pl.ds(start, size), :] = unit_heads(part)
+            else:
+                vt_ref[:, pl.ds(start, size)] = part.astype(BF16).T
+
+    inner = [(margin + i * nodes, nodes) for i in range(2)]
+    edges = [(i * (margin + 2 * nodes), margin) for i in range(2)]
 
     head_of = lax.broadcasted_iota(jnp.int32, (nodes, gw), 1) // head_size
 
@@ -296,93 +324,67 @@
         return remote(att_ref.at[parts + g], att_ref.at[at], give_send.at[g], give_recv.at[g],
                       (d, partner))
 
-    def at_group(g, value, action):
-        @pl.when(g == value)
-        def _():
-            action()
-
-    @pl.loop(0, groups)
-    def _(g):
-        for value in range(groups):
-            at_group(g, value, lambda: finish(3 * value + 1))
-        keys(g, own_edge)
-
-        @pl.when(g == 0)
-        def _():
-            norm_copy(0, far_base, nodes).wait_recv()
-            norm_copy(1, far_halo, margin).wait_recv()
-
-        keys(g, far_edge)
-        for value in range(groups):
-            at_group(g, value, lambda: finish(3 * value))
-        for i in range(2):
-            queries(g, i)
-        at_group(g, 0, lambda: relay(order[3]))
-        for value in range(groups):
-            at_group(g, value, lambda: finish(3 * value + 2))
-        values(g, own_edge)
-        values(g, far_edge)
-        at_group(g, 1, lambda: relay(order[6]))
-
-        @pl.loop(0, 2)
-        def _(i):
-            t = jnp.where(i == 0, 1 - core, core)
-            attend(t, jnp.where(i == 0, parts + g, core * groups + g))
-
-            @pl.when(i == 0)
-            def _():
-                for value in range(groups):
-                    at_group(g, value, lambda: give(value, True).start())
-
-                at_group(g, 0, lambda: relay(order[4]))
-
-                @pl.when(g == groups - 1)
-                def _():
-                    relay(order[7])
-                    finish(order[6])
-                    swap(groups * core).start()
-
-            @pl.when((i == 1) & (g == 0))
-            def _():
-                relay(order[5])
-
+    def leave(j):
+        columns = pl.ds(pl.multiple_of(j * gw, gw), gw)
+        update_ref[:, columns] = sum(
+            jnp.dot(att_ref[at], wo_ref[j, pl.ds(at * gw, gw), :], preferred_element_type=F32)
+            for at in range(parts)).astype(BF16)
+
+    finish(1)
+    run(0, [(1, own_base, nodes)])
+    for i in range(2):
+        norm_copy(i, far_base + i * margin, margin).wait_recv()
+    run(0, [(1, far_base, nodes)])
+    finish(0)
+    run(0, [(0, *at) for at in inner])
+    relay(order[3])
+    embed_halo()
+    finish(2)
+    relay(order[4])
+    run(0, [(2, *at) for at in inner])
+    norm_copy(2, far_halo, margin).wait_recv()
+    run(0, [(1, *at) for at in edges] + [(2, *at) for at in edges])
+    attend(1 - core, parts)
+    give(0, True).start()
+    relay(order[5])
+    attend(core, core * groups)
+
+    finish(4)
+    finish(3)
+    run(1, [(1, *at) for at in inner] + [(0, *at) for at in inner])
+    relay(order[6])
+    finish(5)
+    run(1, [(1, *at) for at in edges] + [(2, *at) for at in inner + edges])
+    attend(1 - core, parts + 1)
+    give(1, True).start()
+    finish(order[6])
+    swap(groups * core).start()
     finish(order[7])
     swap(groups * core + 1).start()
+    attend(core, core * groups + 1)
+
     for g in range(groups):
         give(g, False).wait_recv()
         swap(groups * (1 - core) + g).wait_recv()
-    for copy in (field_up, field_down, enc_copy(far_halo), norm_copy(0, own_base, nodes),
-                 norm_copy(1, own_halo, margin)):
+    for j in range(parts):
+        leave(j)
+    for copy in (field_up, field_down, enc_copy(far_halo), norm_copy(0, own_base, margin),
+                 norm_copy(1, own_base + margin, margin), norm_copy(2, own_halo, margin)):
         copy.wait_send()
     for g in range(groups):
         give(g, True).wait_send()
         swap(groups * core + g).wait_send()
     for c in order:
-        for i in range(n - 1):
-            direct(c, i, d).wait_send()
-            if share:
-                onward(c, i, True).wait_send()
-
-
-def project(enc_ref, w_in_ref, att_ref, w_out_ref, latent_hbm, update_hbm,
-            latent_ref, update_ref, latent_sem, update_sem):
-    parts, _, gw = w_out_ref.shape
-    half = enc_ref.shape[0] // 2
-    copies = []
-    for i in range(2):
-        span = pl.ds(i * half, half)
-        latent_ref[span, :] = jnp.dot(
-            enc_ref[span, :], w_in_ref[...], preferred_element_type=F32).astype(BF16)
-        copies.append(pltpu.make_async_copy(
-            latent_ref.at[span, :], latent_hbm.at[span, :], latent_sem.at[i]))
-        copies[-1].start()
-    for j in range(parts):
-        update_ref[j] = sum(
-            jnp.dot(att_ref[g], w_out_ref[j, pl.ds(g * gw, gw), :], preferred_element_type=F32)
-            for g in range(parts)).astype(BF16)
-        copies.append(pltpu.make_async_copy(
-            update_ref.at[j], update_hbm.at[:, pl.ds(j * gw, gw)], update_sem.at[j]))
-        copies[-1].start()
+        all_direct(c).wait_send()
+        if level[c]:
+            all_onward(c).wait_send()
+
+
+def deliver(latent_ref, update_ref, latent_hbm, update_hbm, sem):
+    copies = [pltpu.make_async_copy(update_ref, update_hbm, sem.at[0]),
+              pltpu.make_async_copy(latent_ref, latent_hbm, sem.at[1])]
+    for copy in copies:
+        copy.start()
     for copy in copies:
         copy.wait()
 
@@ -400,13 +402,11 @@
     vmem = pl.BlockSpec(memory_space=pltpu.VMEM)
     hbm = pl.BlockSpec(memory_space=pl.ANY)
     dma = pltpu.SemaphoreType.DMA
-    attended, w_out_full, encoded, w_in_full = pl.pallas_call(
+    results = pl.pallas_call(
         functools.partial(kernel, n, space),
-        out_shape=[pltpu.VMEM(shape, BF16)
-                   for shape in ((parts + groups, nodes, gw), (parts, width, gw),
-                                 (nodes, 128), (128, width))],
+        out_shape=[pltpu.VMEM((nodes, width), BF16)] * 2,
         in_specs=[hbm] * 7,
-        out_specs=[vmem] * 4,
+        out_specs=[vmem] * 2,
         scratch_shapes=[
             pltpu.SMEM(cell_index.shape, jnp.int32),
             pltpu.VMEM((channels, cells), BF16),
@@ -418,15 +418,17 @@
             pltpu.VMEM((cells + 2 * reach, 128), F32),
             pltpu.VMEM((blocks * 128, 128), F32),
             pltpu.VMEM((3 * nodes, 128), BF16),
+            pltpu.VMEM((128, width), BF16),
             pltpu.VMEM((3 * nodes, width), BF16),
             pltpu.VMEM((3 * groups, width, gw), BF16),
             pltpu.VMEM((2 * nodes, gw), BF16),
             pltpu.VMEM((3 * nodes, gw), BF16),
             pltpu.VMEM((gw, 3 * nodes), BF16),
+            pltpu.VMEM((parts + groups, nodes, gw), BF16),
+            pltpu.VMEM((parts, width, gw), BF16),
             dma((5,)), dma((chunks,)),
-            dma((2,)), dma((2,)), dma((1,)), dma((1,)), dma((2,)), dma((2,)),
-            dma((chunks, n - 1)), dma((chunks, n - 1)),
-            dma((chunks, 3)), dma((chunks, 3)),
+            dma((2,)), dma((2,)), dma((1,)), dma((1,)), dma((3,)), dma((3,)),
+            dma((chunks,)), dma((chunks,)), dma((chunks,)), dma((chunks,)),
             dma((groups,)), dma((groups,)), dma((groups,)), dma((groups,)),
         ],
         compiler_params=pltpu.CompilerParams(
@@ -434,19 +436,14 @@
     )(*[pltpu.with_memory_space_constraint(array, pltpu.HBM) for array in (
         cell_index, fields[0], interp_weight, w_in, ln_gain[None], w_qkv, w_out)])
 
-    operands = [pltpu.with_memory_space_constraint(array, pltpu.VMEM)
-                for array in (encoded, w_in_full, attended, w_out_full)]
     latent, update = pl.pallas_call(
-        project,
+        deliver,
         out_shape=[jax.ShapeDtypeStruct((nodes, width), BF16)] * 2,
-        in_specs=[vmem] * 4,
+        in_specs=[vmem] * 2,
         out_specs=[hbm] * 2,
-        scratch_shapes=[
-            pltpu.VMEM((nodes, width), BF16), pltpu.VMEM((parts, nodes, gw), BF16),
-            dma((2,)), dma((parts,)),
-        ],
-        compiler_params=pltpu.CompilerParams(vmem_limit_bytes=16 * 2**20),
-    )(*operands)
+        scratch_shapes=[dma((2,))],
+        compiler_params=pltpu.CompilerParams(vmem_limit_bytes=2**20),
+    )(*[pltpu.with_memory_space_constraint(array, pltpu.VMEM) for array in results])
     return latent[None], update[None]
 
 

time: 54.1 us -> 43.9 us (0.81)
  Pallas kernels: 53.4 us -> 42.9 us
    pallas_call x1, Pallas kernels: 51 us -> 41.6 us  [shards(): pl.pallas_call(functools.partial(kernel, n, space), out_shape=[pltpu.VMEM...]
    pallas_call x1, Pallas kernels: 2.37 us -> 1.33 us  [shards(): pl.pallas_call(deliver, out_shape=[jax.ShapeDtypeStruct((nodes, width), B...]
where the time goes in v2:
time: 43.9 us; the launch traced here: 43.7 us
  Pallas kernels  42.9 us (98%)
  between operations  0.8 us (2%)
    pallas_call x1, Pallas kernels, shards(): pl.pallas_call(functools.partial(kernel, n, space), out_shape=[pltpu.VMEM...  41.6 us
    pallas_call x1, Pallas kernels, shards(): pl.pallas_call(deliver, out_shape=[jax.ShapeDtypeStruct((nodes, width), B...  1.33 us

profile of v2, /device:TPU:0, one launch (start us, length us, event | category | flops | bytes accessed | tf_op | source)
XLA Modules:
  0.0 43.7 jit_solution(17481584547612447511)
XLA Ops:
  0.6 41.6 %shard_map.86 = (bf16[512,1024]{1,0:T(8,128)(2,1)S(1)}, bf16[512,1024]{1,0:T(8,128)(2,1)S(1)}) custom-call(s32[32,128]{1,0:T(8,128)} %index_hbm.1, bf16[100,4096]{1,0:T(8,128)(2,1)} %bitcast.4, bf16[32,16,128]{2,1,0:T(8,128)(2,1)} %weight_hbm.1, bf16[100,1024]{1,0:T(8,128)(2,1)} %w_in_hbm.1, f32[1,1024]{1,0:T(1,128)} %bitcast.5, ...), custom_call_target="tpu_custom_call" | custom-call | tf_op jit(solution)/shard_map/pallas_call | solution.py:405
  42.2 1.3 %shard_map.87 = (bf16[512,1024]{1,0:T(8,128)(2,1)}, bf16[512,1024]{1,0:T(8,128)(2,1)}) custom-call(bf16[512,1024]{1,0:T(8,128)(2,1)S(1)} %get-tuple-element.6.latent_ref, bf16[512,1024]{1,0:T(8,128)(2,1)S(1)} %get-tuple-element.7.update_ref), custom_call_target="tpu_custom_call" | custom-call | tf_op jit(solution)/shard_map/pallas_call | solution.py:439

commit v3 on v2

--- a/solution.py
+++ b/solution.py
@@ -20,7 +20,7 @@
     latent_ref, update_ref,
     index_ref, field_ref, weight_ref, w_in_ref, gain_ref,
     low_ref, high_ref, cells_ref, picked_ref, enc_ref, w_in_full, normed_ref, wq_ref,
-    q_ref, k_ref, vt_ref, att_ref, wo_ref,
+    q_ref, k_ref, vt_ref, att_ref, wo_ref, weight_of, total_ref,
     in_sem, local_sem, field_send, field_recv, enc_send, enc_recv, norm_send, norm_recv,
     a_send, a_recv, z_send, z_recv, swap_send, swap_recv, give_send, give_recv,
 ):
@@ -298,26 +298,41 @@
 
     head_of = lax.broadcasted_iota(jnp.int32, (nodes, gw), 1) // head_size
 
-    def attend(t, slot):
+    def weigh(t, h):
         start = pl.multiple_of(t * nodes, nodes)
         asked = q_ref[pl.ds(start, nodes), :]
-        seen = pl.ds(start, window)
-
-        def score(h):
-            picked = jnp.where(head_of == h, asked, jnp.zeros_like(asked))
-            return lax.dot_general(k_ref[seen, :], picked, CONTRACT_LAST, preferred_element_type=F32)
-
+        picked = jnp.where(head_of == h, asked, jnp.zeros_like(asked))
+        return jnp.exp(lax.dot_general(
+            k_ref[pl.ds(start, window), :], picked, CONTRACT_LAST, preferred_element_type=F32))
+
+    def mix(t, h, weights, total):
+        seen = pl.ds(pl.multiple_of(t * nodes, nodes), window)
+        return jnp.dot(vt_ref[pl.ds(h * head_size, head_size), seen], weights,
+                       preferred_element_type=F32) * (1.0 / total)
+
+    def settle(slot, h, outs):
+        att_ref[slot, :, h * head_size:(h + len(outs)) * head_size] = (
+            jnp.concatenate(outs, axis=0).astype(BF16).T)
+
+    def attend(t, slot, heads=range(GROUP_HEADS)):
         outs = []
-        scores = score(0)
+        weights = weigh(t, heads[0])
+        for h in heads:
+            later = weigh(t, h + 1) if h + 1 < heads.stop else None
+            total = jnp.sum(weights, axis=0, keepdims=True)
+            outs.append(mix(t, h, weights.astype(BF16), total))
+            weights = later
+        settle(slot, heads[0], outs)
+
+    def prepare(t):
         for h in range(GROUP_HEADS):
-            weights = jnp.exp(scores)
-            if h + 1 < GROUP_HEADS:
-                scores = score(h + 1)
-            total = jnp.sum(weights, axis=0, keepdims=True)
-            out = jnp.dot(vt_ref[pl.ds(h * head_size, head_size), seen], weights.astype(BF16),
-                          preferred_element_type=F32)
-            outs.append(out * (1.0 / total))
-        att_ref[slot] = jnp.concatenate(outs, axis=0).astype(BF16).T
+            weights = weigh(t, h)
+            total_ref[pl.ds(h, 1), :] = jnp.sum(weights, axis=0, keepdims=True)
+            weight_of[h] = weights.astype(BF16)
+
+    def conclude(t, slot):
+        settle(slot, 0, [mix(t, h, weight_of[h], total_ref[pl.ds(h, 1), :])
+                         for h in range(GROUP_HEADS)])
 
     def give(g, mine):
         at = core * groups + g if mine else (1 - core) * groups + g
@@ -339,12 +354,13 @@
     run(0, [(0, *at) for at in inner])
     relay(order[3])
     embed_halo()
+    norm_copy(2, far_halo, margin).wait_recv()
+    run(0, [(1, *at) for at in edges])
+    relay(order[4])
+    prepare(1 - core)
     finish(2)
-    relay(order[4])
-    run(0, [(2, *at) for at in inner])
-    norm_copy(2, far_halo, margin).wait_recv()
-    run(0, [(1, *at) for at in edges] + [(2, *at) for at in edges])
-    attend(1 - core, parts)
+    run(0, [(2, *at) for at in inner + edges])
+    conclude(1 - core, parts)
     give(0, True).start()
     relay(order[5])
     attend(core, core * groups)
@@ -426,6 +442,8 @@
             pltpu.VMEM((gw, 3 * nodes), BF16),
             pltpu.VMEM((parts + groups, nodes, gw), BF16),
             pltpu.VMEM((parts, width, gw), BF16),
+            pltpu.VMEM((GROUP_HEADS, 2 * nodes, nodes), BF16),
+            pltpu.VMEM((8, nodes), F32),
             dma((5,)), dma((chunks,)),
             dma((2,)), dma((2,)), dma((1,)), dma((1,)), dma((3,)), dma((3,)),
             dma((chunks,)), dma((chunks,)), dma((chunks,)), dma((chunks,)),

time: 43.9 us -> 43.9 us (level)
  no operation moved by 1% of the time
where the time goes in v3:
time: 43.9 us; the launch traced here: 43.7 us
  Pallas kernels  42.9 us (98%)
  between operations  0.8 us (2%)
    pallas_call x1, Pallas kernels, shards(): pl.pallas_call(functools.partial(kernel, n, space), out_shape=[pltpu.VMEM...  41.6 us
    pallas_call x1, Pallas kernels, shards(): pl.pallas_call(deliver, out_shape=[jax.ShapeDtypeStruct((nodes, width), B...  1.33 us

profile of v3, /device:TPU:0, one launch (start us, length us, event | category | flops | bytes accessed | tf_op | source)
XLA Modules:
  0.0 43.7 jit_solution(11906225262770972662)
XLA Ops:
  0.6 41.6 %shard_map.86 = (bf16[512,1024]{1,0:T(8,128)(2,1)S(1)}, bf16[512,1024]{1,0:T(8,128)(2,1)S(1)}) custom-call(s32[32,128]{1,0:T(8,128)} %index_hbm.1, bf16[100,4096]{1,0:T(8,128)(2,1)} %bitcast.4, bf16[32,16,128]{2,1,0:T(8,128)(2,1)} %weight_hbm.1, bf16[100,1024]{1,0:T(8,128)(2,1)} %w_in_hbm.1, f32[1,1024]{1,0:T(1,128)} %bitcast.5, ...), custom_call_target="tpu_custom_call" | custom-call | tf_op jit(solution)/shard_map/pallas_call | solution.py:421
  42.2 1.3 %shard_map.87 = (bf16[512,1024]{1,0:T(8,128)(2,1)}, bf16[512,1024]{1,0:T(8,128)(2,1)}) custom-call(bf16[512,1024]{1,0:T(8,128)(2,1)S(1)} %get-tuple-element.6.latent_ref, bf16[512,1024]{1,0:T(8,128)(2,1)S(1)} %get-tuple-element.7.update_ref), custom_call_target="tpu_custom_call" | custom-call | tf_op jit(solution)/shard_map/pallas_call | solution.py:457
